TPU v7x, 1024 devices: a whole 8x8x8 slice. The times are simulated.
1024 devices in a mesh: prompt: 16 (over x, core), sample: 64 (over y, z).
Axes of the slice: x: 8, y: 8, z: 8, core: 2. Of those that a mesh axis runs over, the one named last changes fastest.
Arguments:
- latent: bfloat16 [1024, 576], P('prompt'), may hold values from -16 to 16
- queries: bfloat16 [4096, 128, 576], P('prompt', 'sample'), may hold values from -64 to 64
- cotangent: bfloat16 [4096, 128, 512], P('prompt', 'sample'), may hold values from -18 to 18
- suffix_out: bfloat16 [4096, 128, 512], P('prompt', 'sample'), may hold values from -6 to 6
- suffix_lse: bfloat16 [4096, 128], P('prompt', 'sample'), may hold values from 6 to 10
- rewards: float32 [16], replicated, may hold values from -5 to 5
- slot_sample: int32 [4096], P('prompt'), may hold values from 0 to 16, as said below
Outputs:
- query_grad: bfloat16 [4096, 128, 576], P('prompt', 'sample')
- latent_grad: float32 [1024, 576], P('prompt')
Inputs may be any that keep to these rules, and one draw needn't show every extreme that they name: `slot_sample`: on every device the live slots come first and the others hold 16. Read over the devices in order, the live slots' completion numbers never fall, and every completion has a slot. Exactly 2048 slots are live in all, and some device has all 256 of its slots live.
All inputs are finite; a program needn't handle non-finite values.
Results may differ from a plain program's by a relative error of at most 0.006.
Values may be sent and summed in bfloat16 or wider, within the bound.
No kernel may reach another device: no remote copies, remote signals or barrier semaphores. Data moves between devices by JAX's collectives and lax.ppermute only.
A program may use at most 32 MiB of HBM per device.

v0:
```python
import math

import jax
import jax.numpy as jnp
from jax import lax
from jax.sharding import PartitionSpec as P

ROPE = 64
NOPE = 128


def copy_for_each(shard, axis):
    devices = lax.axis_size(axis)
    return lax.all_to_all(
        jnp.broadcast_to(shard[None], (devices, *shard.shape)), axis, 0, 0, tiled=True
    )


def laid_out(pieces, dim):
    lengths = list(pieces.shape[1:])
    lengths[dim] *= pieces.shape[0]
    return jnp.moveaxis(pieces, 0, dim).reshape(lengths)


def gathered_copies(shard, axis, dim):
    pieces = copy_for_each(shard, axis)
    return laid_out(pieces, dim)


def cut_along(shard, dim, devices):
    lengths = shard.shape
    pieces = shard.reshape(*lengths[:dim], devices, lengths[dim] // devices, *lengths[dim + 1 :])
    return jnp.moveaxis(pieces, dim, 0)


def sent_and_summed(shard, axis, dim):
    devices = lax.axis_size(axis)
    pieces = lax.all_to_all(cut_along(shard, dim, devices), axis, 0, 0, tiled=True)
    return jnp.sum(pieces, axis=0)


def softmax_scale():
    return (0.1 * math.log(40.0) + 1.0) ** 2 / math.sqrt(NOPE + ROPE)


def attend(queries, scaled, suffix_out, suffix_lse, prefix_keys, factor):
    value_width = scaled.shape[-1]
    scores = factor * jnp.einsum(
        "thd,pd->thp", queries, prefix_keys, preferred_element_type=jnp.float32
    )
    row_max = jnp.max(scores, axis=2)
    prefix_lse = row_max + jnp.log(jnp.sum(jnp.exp(scores - row_max[..., None]), axis=2))
    tail_lse = suffix_lse.astype(jnp.float32)
    joint_max = jnp.maximum(prefix_lse, tail_lse)
    total_lse = joint_max + jnp.log(jnp.exp(prefix_lse - joint_max) + jnp.exp(tail_lse - joint_max))
    probability = jnp.exp(scores - total_lse[..., None])
    prob_grad = jnp.einsum(
        "thd,pd->thp", scaled, prefix_keys[:, :value_width], preferred_element_type=jnp.float32
    )
    suffix_dot = jnp.sum(scaled.astype(jnp.float32) * suffix_out.astype(jnp.float32), axis=2)
    row_delta = (
        jnp.sum(probability * prob_grad, axis=2) + jnp.exp(tail_lse - total_lse) * suffix_dot
    )
    score_grad = (factor * probability * (prob_grad - row_delta[..., None])).astype(jnp.bfloat16)
    weights = probability.astype(jnp.bfloat16)
    query_grad = jnp.einsum(
        "thp,pd->thd", score_grad, prefix_keys, preferred_element_type=jnp.float32
    ).astype(jnp.bfloat16)

    def term_rows(first_row, row_count):
        key_term = jnp.einsum(
            "thp,thd->pd", score_grad, queries, preferred_element_type=jnp.float32
        )
        value_term = jnp.einsum("thp,thd->pd", weights, scaled, preferred_element_type=jnp.float32)
        return key_term + jnp.pad(value_term, ((0, 0), (0, key_term.shape[1] - value_width)))

    return (query_grad, term_rows)


def on_device(latent, queries, cotangent, suffix_out, suffix_lse, rewards, slot_sample):
    factor = softmax_scale()
    prefix_keys = gathered_copies(latent, "prompt", 0)
    centred = rewards - jnp.mean(rewards)
    advantage_table = jnp.concatenate([centred, jnp.zeros((1,), jnp.float32)])
    sample_ids = jnp.arange(advantage_table.shape[0], dtype=jnp.int32)
    weight = jnp.sum(
        jnp.where(slot_sample[:, None] == sample_ids[None, :], advantage_table[None, :], 0.0),
        axis=1,
    )
    scaled = (weight[:, None, None] * cotangent.astype(jnp.float32)).astype(jnp.bfloat16)
    query_grad, term_rows = attend(queries, scaled, suffix_out, suffix_lse, prefix_keys, factor)
    prefix_count = prefix_keys.shape[0]
    owner_sums = sent_and_summed(term_rows(0, prefix_count), "prompt", 0)
    latent_grad = lax.psum(owner_sums, "sample")
    return (query_grad, latent_grad)


def solution(mesh):
    in_specs = (
        P("prompt", None),
        P("prompt", "sample", None),
        P("prompt", "sample", None),
        P("prompt", "sample", None),
        P("prompt", "sample"),
        P(),
        P("prompt"),
    )
    out_specs = (P("prompt", "sample", None), P("prompt", None))
    return jax.shard_map(
        on_device, mesh=mesh, in_specs=in_specs, out_specs=out_specs, check_vma=False
    )
```

profile of v0, /device:TPU:2, one launch (start us, length us, event | category | flops | bytes accessed | tf_op | source)
XLA Modules:
  0.0 308.1 jit_solution(14832719972328768206)
XLA Ops:
  7.2 2.2 broadcast_in_dim.10
  9.4 16.7 %all-to-all-start = ((bf16[16,64,576]{2,1,0:T(8,128)(2,1)}), bf16[16,64,576]{2,1,0:T(8,128)(2,1)S(1)}, u32[]{:S(2)}, u32[]{:S(2)}) async-start(bf16[16,64,576]{2,1,0:T(8,128)(2,1)} %broadcast_in_dim.10), calls=%async_computation | async-start | bytes 2621440 | tf_op jit(solution)/shard_map/all_to_all | solution.py:14
  26.1 0.0 all-reduce.3.cloned.1.call-start
  26.1 0.6 reduce_sum.55
  27.4 0.1 pad_maximum_fusion
  27.5 0.1 select_reduce_fusion
  27.6 2.0 multiply_reduce_fusion.2
  29.6 0.5 copy.39
  30.1 1.0 copy.37
  31.1 25.2 %all-to-all-done = bf16[16,64,576]{2,1,0:T(8,128)(2,1)S(1)} async-done(((bf16[16,64,576]{2,1,0:T(8,128)(2,1)}), bf16[16,64,576]{2,1,0:T(8,128)(2,1)S(1)}, u32[]{:S(2)}, u32[]{:S(2)}) %all-to-all-start) | async-done | bytes 1179680 | tf_op jit(solution)/shard_map/all_to_all | solution.py:14
  56.3 1.1 multiply_reduce_fusion.1
  57.4 0.5 exponential_reduce_fusion
  58.0 0.9 convolution_bitcast_fusion
  58.9 1.2 multiply_reduce_fusion
  60.1 0.6 multiply_convert_fusion
  60.7 1.0 copy-done.2
  61.7 0.8 bitcast_add_fusion
  62.5 2.1 copy.40
  64.6 66.0 %all_to_all.10 = f32[16,64,576]{2,1,0:T(8,128)S(1)} all-to-all(f32[16,64,576]{2,1,0:T(8,128)} %bitcast.22), channel_id=1, replica_groups=mesh['prompt'=16,'sample'=64] {'prompt'}, dimensions={0} | all-to-all | bytes 4718592 | tf_op jit(solution)/shard_map/all_to_all | solution.py:38
  130.6 0.8 reduce_sum.59
  131.4 0.0 all-reduce.3.cloned.1.call-update
  131.4 3.3 %convolution_convert_fusion = bf16[256,2,576]{0,2,1:T(8,128)(2,1)} fusion(bf16[256,2,1024]{2,0,1:T(8,128)(2,1)} %copy-done.2, bf16[1024,576,1]{1,0,2:T(8,128)(2,1)} %bitcast.25), kind=kOutput, calls=%fused_computation.8 | convolution fusion | flops 604274688 | bytes 2818048 | tf_op jit(solution)/shard_map/thp,pd->thd/dot_general | solution.py:66
  134.7 164.9 %all-reduce.3.cloned.1.call-done = f32[64,576]{1,0:T(8,128)} async-done(((f32[64,576]{1,0:T(8,128)}), f32[64,576]{1,0:T(8,128)}) %all-reduce.3.cloned.1.call-update) | async-done | bytes 147472 | tf_op jit(solution)/shard_map/psum | solution.py:94
  299.6 1.6 copy.46
  (18 shorter events, 0.1 us)
Async XLA Ops:
  7.2 49.1 %copy-start = (bf16[256,2,576]{0,2,1:T(8,128)(2,1)S(1)}, bf16[256,2,576]{0,2,1:T(8,128)(2,1)}, u32[]{:S(2)}) copy-start(bf16[256,2,576]{0,2,1:T(8,128)(2,1)} %param.8) | copy-start | bytes 1769476
  7.2 19.0 %copy-start.7 = (f32[16]{0:T(128)S(1)}, f32[16]{0:T(128)}, u32[]{:S(2)}) copy-start(f32[16]{0:T(128)} %param.12) | copy-start | bytes 196
  7.2 20.3 %copy-start.6 = (s32[256]{0:T(256)S(1)}, s32[256]{0:T(256)}, u32[]{:S(2)}) copy-start(s32[256]{0:T(256)} %param.13) | copy-start | bytes 3076
  7.2 20.4 %copy-start.3 = (bf16[256,2,512]{2,1,0:T(2,128)(2,1)S(1)}, bf16[256,2,512]{2,1,0:T(2,128)(2,1)}, u32[]{:S(2)}) copy-start(bf16[256,2,512]{2,1,0:T(2,128)(2,1)} %param.10) | copy-start | bytes 1572868
  7.2 20.4 %copy-start.4 = (bf16[256,2,512]{2,1,0:T(2,128)(2,1)S(1)}, bf16[256,2,512]{2,1,0:T(2,128)(2,1)}, u32[]{:S(2)}) copy-start(bf16[256,2,512]{2,1,0:T(2,128)(2,1)} %param.9) | copy-start | bytes 1572868
  9.4 46.9 %all-to-all-start = ((bf16[16,64,576]{2,1,0:T(8,128)(2,1)}), bf16[16,64,576]{2,1,0:T(8,128)(2,1)S(1)}, u32[]{:S(2)}, u32[]{:S(2)}) async-start(bf16[16,64,576]{2,1,0:T(8,128)(2,1)} %broadcast_in_dim.10), calls=%async_computation | async-start | bytes 2621440 | tf_op jit(solution)/shard_map/all_to_all | solution.py:14
  26.1 273.5 %all-reduce.3.cloned.1.call-start = ((), (), s32[]{:S(2)}) async-start(), calls=%async_computation.2 | async-start | bytes 327680 | tf_op jit(solution)/shard_map/psum | solution.py:94
  56.3 2.6 copy-start.1
  56.3 1.6 copy-start.5
  60.7 1.0 copy-start.2
Sparse Core Ops, SparseCore 0:
  131.6 168.0 all-reduce.2
where the time goes:
time: 308 us
  waiting for transfers between devices  190 us (62%)
  blocking collectives  66 us (21%)
  starting transfers between devices  16.7 us (5%)
  between operations  14.8 us (5%)
  local copies, waits for them, and re-layouts  8.42 us (3%)
  matrix products  7.25 us (2%)
  other arithmetic  4.75 us (2%)
    psum x1, waiting for transfers between devices, on_device(): latent_grad = lax.psum(owner_sums, 'sample')  165 us
    all_to_all x1, blocking collectives, sent_and_summed(): lax.all_to_all(cut_along(shard, dim, devices), axis, 0, 0, tiled=True)  66 us
    all_to_all x1, waiting for transfers between devices, copy_for_each(): lax.all_to_all(jnp.broadcast_to(shard[None], (devices, *shard.shape)), ax...  25.2 us
    all_to_all x1, starting transfers between devices, copy_for_each(): lax.all_to_all(jnp.broadcast_to(shard[None], (devices, *shard.shape)), ax...  16.7 us
  transfers between devices with their start and end apart: 2, of which 2 were waited for; matrix products, arithmetic and copies ran while one was open for 2% of the time, Pallas kernels for 0%

commit v1 on v0

v1 whole, which is shorter than its diff:
```python
import math

import jax
import jax.numpy as jnp
from jax import lax
from jax.sharding import Mesh, PartitionSpec as P

ROPE = 64
NOPE = 128


def softmax_scale():
    return (0.1 * math.log(40.0) + 1.0) ** 2 / math.sqrt(NOPE + ROPE)


def to_partner(value):
    return lax.ppermute(value, "core", [(0, 1), (1, 0)])


def exchanged(pieces, axes):
    return lax.all_to_all(pieces, axes, 0, 0, tiled=True)


def attend(queries, scaled, suffix_dot, suffix_lse, keys, factor):
    value_width = scaled.shape[-1]
    scores = factor * jnp.einsum("thd,pd->htp", queries, keys, preferred_element_type=jnp.float32)
    row_max = jnp.max(scores, axis=2)
    prefix_lse = row_max + jnp.log(jnp.sum(jnp.exp(scores - row_max[..., None]), axis=2))
    tail_lse = suffix_lse.astype(jnp.float32).T
    joint_max = jnp.maximum(prefix_lse, tail_lse)
    total_lse = joint_max + jnp.log(jnp.exp(prefix_lse - joint_max) + jnp.exp(tail_lse - joint_max))
    probability = jnp.exp(scores - total_lse[..., None])
    prob_grad = jnp.einsum(
        "thd,pd->htp", scaled, keys[:, :value_width], preferred_element_type=jnp.float32
    )
    row_delta = (
        jnp.sum(probability * prob_grad, axis=2) + jnp.exp(tail_lse - total_lse) * suffix_dot.T
    )
    score_grad = (factor * probability * (prob_grad - row_delta[..., None])).astype(jnp.bfloat16)
    weights = probability.astype(jnp.bfloat16)

    def query_grad():
        return jnp.einsum(
            "htp,pd->thd", score_grad, keys, preferred_element_type=jnp.float32
        ).astype(jnp.bfloat16)

    def key_grad(first, count):
        rows = slice(first, first + count)
        key_term = jnp.einsum(
            "htp,thd->pd", score_grad[..., rows], queries, preferred_element_type=jnp.float32
        )
        value_term = jnp.einsum(
            "htp,thd->pd", weights[..., rows], scaled, preferred_element_type=jnp.float32
        )
        return key_term + jnp.pad(value_term, ((0, 0), (0, key_term.shape[1] - value_width)))

    return query_grad, key_grad


def on_device(latent, queries, cotangent, suffix_out, suffix_lse, rewards, slot_sample):
    factor = softmax_scale()
    chips = lax.axis_size("x")
    ys, zs = lax.axis_size("y"), lax.axis_size("z")
    rows, width = latent.shape
    half = chips * rows

    mine = exchanged(jnp.broadcast_to(latent[None], (chips, rows, width)), "x").reshape(half, width)
    keys = jnp.concatenate([mine, to_partner(mine)], axis=0)

    centred = rewards - jnp.mean(rewards)
    advantage_table = jnp.concatenate([centred, jnp.zeros((1,), jnp.float32)])
    sample_ids = jnp.arange(advantage_table.shape[0], dtype=jnp.int32)
    weight = jnp.sum(
        jnp.where(slot_sample[:, None] == sample_ids[None, :], advantage_table[None, :], 0.0),
        axis=1,
    )
    scaled = (weight[:, None, None] * cotangent.astype(jnp.float32)).astype(jnp.bfloat16)
    suffix_dot = jnp.sum(scaled.astype(jnp.float32) * suffix_out.astype(jnp.float32), axis=2)

    query_grad, key_grad = attend(queries, scaled, suffix_dot, suffix_lse, keys, factor)
    received = to_partner(key_grad(half, half))
    on_chip = (key_grad(0, half) + received).astype(jnp.bfloat16)

    pieces = exchanged(on_chip.reshape(chips * ys, rows // ys, width), ("x", "y"))
    part = jnp.sum(pieces.astype(jnp.float32), axis=0).astype(jnp.bfloat16)
    copies = exchanged(jnp.broadcast_to(part[None], (ys * zs, *part.shape)), ("y", "z"))
    copies = copies.reshape(ys, zs, rows // ys, width).astype(jnp.float32)
    latent_grad = jnp.sum(copies, axis=1).reshape(rows, width)
    return query_grad(), latent_grad


def solution(mesh):
    prompt, sample = mesh.devices.shape
    side = math.isqrt(sample)
    grid = Mesh(
        mesh.devices.reshape(prompt // 2, 2, side, sample // side), ("x", "core", "y", "z")
    )
    slots, heads = ("x", "core"), ("y", "z")
    in_specs = (
        P(slots, None),
        P(slots, heads, None),
        P(slots, heads, None),
        P(slots, heads, None),
        P(slots, heads),
        P(),
        P(slots),
    )
    out_specs = (P(slots, heads, None), P(slots, None))
    return jax.shard_map(
        on_device, mesh=grid, in_specs=in_specs, out_specs=out_specs, check_vma=False
    )
```

time: 308 us -> 121 us (0.39)
  the two profiles are of different devices: /device:TPU:2 before, /device:TPU:32 now
where the time goes in v1:
time: 121 us; the launch traced here: 120 us
  waiting for transfers between devices  38.8 us (32%)
  starting transfers between devices  32.9 us (27%)
  blocking collectives  29.5 us (24%)
  matrix products  8.79 us (7%)
  other arithmetic  4.63 us (4%)
  local copies, waits for them, and re-layouts  4.27 us (4%)
  between operations  1.48 us (1%)
    all_to_all x2, waiting for transfers between devices, exchanged(): return lax.all_to_all(pieces, axes, 0, 0, tiled=True)  36.8 us
    all_to_all x1, blocking collectives, exchanged(): return lax.all_to_all(pieces, axes, 0, 0, tiled=True)  29.5 us
    all_to_all x2, starting transfers between devices, exchanged(): return lax.all_to_all(pieces, axes, 0, 0, tiled=True)  28.6 us
    ppermute x2, starting transfers between devices, to_partner(): return lax.ppermute(value, 'core', [(0, 1), (1, 0)])  4.33 us
    dot_general x1, matrix products, query_grad(): jnp.einsum('htp,pd->thd', score_grad, keys, preferred_element_type=jnp.fl...  2.84 us
  transfers between devices with their start and end apart: 4, of which 3 were waited for; matrix products, arithmetic and copies ran while one was open for 6% of the time, Pallas kernels for 0%

profile of v1, /device:TPU:32, one launch (start us, length us, event | category | flops | bytes accessed | tf_op | source)
XLA Modules:
  0.0 120.4 jit_solution(12191943127672517079)
XLA Ops:
  0.7 1.9 %broadcast_in_dim.16 = bf16[8,64,576]{2,1,0:T(8,128)(2,1)} broadcast(bf16[64,576]{1,0:T(8,128)(2,1)} %param.7), dimensions={1,2} | broadcast | bytes 663552 | tf_op jit(solution)/shard_map/broadcast_in_dim | solution.py:67
  2.6 6.8 %all-to-all-start = ((bf16[8,64,576]{2,1,0:T(8,128)(2,1)}), bf16[8,64,576]{2,1,0:T(8,128)(2,1)S(1)}, u32[]{:S(2)}, u32[]{:S(2)}) async-start(bf16[8,64,576]{2,1,0:T(8,128)(2,1)} %broadcast_in_dim.16), calls=%async_computation | async-start | bytes 1310720 | tf_op jit(solution)/shard_map/all_to_all | solution.py:21
  9.3 1.3 %reduce_sum.67 = f32[]{:T(128)} reduce(f32[16]{0:T(128)} %param.12, f32[]{:T(128)} %constant.5.clone.1), dimensions={0}, to_apply=%region_2.3 | reduce | flops 15 | bytes 72 | tf_op jit(solution)/shard_map/reduce_sum | solution.py:70
  11.2 18.4 %all-to-all-done = bf16[8,64,576]{2,1,0:T(8,128)(2,1)S(1)} async-done(((bf16[8,64,576]{2,1,0:T(8,128)(2,1)}), bf16[8,64,576]{2,1,0:T(8,128)(2,1)S(1)}, u32[]{:S(2)}, u32[]{:S(2)}) %all-to-all-start) | async-done | bytes 589856 | tf_op jit(solution)/shard_map/all_to_all | solution.py:21
  29.9 1.9 %collective-permute-start = (bf16[512,576]{0,1:T(8,128)(2,1)S(1)}, bf16[512,576]{0,1:T(8,128)(2,1)}, u32[]{:S(2)}, u32[]{:S(2)}) collective-permute-start(bf16[512,576]{0,1:T(8,128)(2,1)S(1)} %copy.61), channel_id=1, source_target_pairs={{0,64},{64,0},{1,65},{65,1},{2,66},{66,2},{3,67},{67,3},{4,68},{68... | collective-permute-start | bytes 1769480 | tf_op jit(solution)/shard_map/ppermute | solution.py:17
  32.0 1.3 %multiply_reduce_fusion = (f32[256,2]{1,0:T(8,128)S(1)}, bf16[256,2,512]{2,1,0:T(2,128)(2,1)S(1)}) fusion(bf16[256,2,512]{2,1,0:T(2,128)(2,1)S(1)} %copy-done.2, bf16[256,2,512]{2,1,0:T(2,128)(2,1)S(1)} %copy-done.3, f32[256]{0:T(256)S(1)} %select_reduce_fusion), kind=kLoop, calls=%fused_computation.30 | loop fusion | flops 1834496 | bytes 1575936 | tf_op jit(solution)/shard_map/reduce_sum | solution.py:78
  33.4 0.5 copy.68
  34.0 2.1 %bitcast_reduce_fusion = (f32[2,256]{1,0:T(2,128)S(1)}, f32[1024,256,2]{1,0,2:T(8,128)S(1)}) fusion(bf16[256,2,576]{0,2,1:T(8,128)(2,1)S(1)} %copy-done, bf16[512,576]{0,1:T(8,128)(2,1)} %collective-permute-done, bf16[512,576]{0,1:T(8,128)(2,1)S(1)} %copy.61), kind=kOutput, calls=%fused_computation.7 | convolution fusion | flops 607387136 | bytes 3868672 | tf_op jit(solution)/shard_map/thd,pd->htp/dot_general | solution.py:26
  36.1 0.4 fusion.4
  36.5 0.3 copy-done.4
  36.8 1.9 %fusion.6 = (bf16[2,256,1024]{1,2,0:T(8,128)(2,1)S(1)}, f32[2,256]{1,0:T(2,128)S(1)}, f32[1024,256,2]{1,0,2:T(8,128)S(1)}) fusion(f32[1024,256,2]{1,0,2:T(8,128)S(1)} %get-tuple-element.7, f32[2,256]{1,0:T(2,128)S(1)} %fusion.28, bf16[256,2,512]{0,2,1:T(8,128)(2,1)S(1)} %copy.68, bf16[512,576]{0,1:T(8,128)(2,1)S(1)} %copy.61, ...), kind=kOutput, calls=%fused_computation.15 | convolution fusion | flops 541588992 | bytes 6950912 | tf_op jit(solution)/shard_map/thd,pd->htp/dot_general | solution.py:33
  38.8 0.5 convolution_bitcast_fusion.2
  39.3 0.6 fusion.2
  39.8 0.5 fusion.9
  40.3 2.4 %collective-permute-start.1 = (f32[512,576]{0,1:T(8,128)S(1)}, f32[512,576]{0,1:T(8,128)S(1)}, u32[]{:S(2)}, u32[]{:S(2)}) collective-permute-start(f32[512,576]{0,1:T(8,128)S(1)} %fusion.9), channel_id=1, source_target_pairs={{0,64},{64,0},{1,65},{65,1},{2,66},{66,2},{3,67},{67,3},{4,68},{68... | collective-permute-start | bytes 3538952 | tf_op jit(solution)/shard_map/ppermute | solution.py:17
  42.7 0.5 convolution_bitcast_fusion.3
  43.2 2.0 %collective-permute-done.1 = f32[512,576]{0,1:T(8,128)S(1)} collective-permute-done((f32[512,576]{0,1:T(8,128)S(1)}, f32[512,576]{0,1:T(8,128)S(1)}, u32[]{:S(2)}, u32[]{:S(2)}) %collective-permute-start.1) | collective-permute-done | bytes 1179680 | tf_op jit(solution)/shard_map/ppermute | solution.py:17
  45.2 0.5 fusion.10
  46.0 29.5 %all_to_all.15 = bf16[64,8,576]{2,1,0:T(8,128)(2,1)S(1)} all-to-all(bf16[64,8,576]{2,1,0:T(8,128)(2,1)S(1)} %bitcast.96), channel_id=1, replica_groups=mesh['x'=8,'core'=2,'y'=8,'z'=8] {'x','y'}, dimensions={0} | all-to-all | bytes 1179648 | tf_op jit(solution)/shard_map/all_to_all | solution.py:21
  75.6 0.9 broadcast_in_dim.19
  76.5 21.9 %all-to-all-start.2 = ((bf16[64,8,576]{2,1,0:T(8,128)(2,1)}), bf16[64,8,576]{2,1,0:T(8,128)(2,1)S(1)}, u32[]{:S(2)}, u32[]{:S(2)}) async-start(bf16[64,8,576]{2,1,0:T(8,128)(2,1)} %broadcast_in_dim.19), calls=%async_computation.2 | async-start | bytes 1310720 | tf_op jit(solution)/shard_map/all_to_all | solution.py:21
  98.4 2.8 %fusion.11 = bf16[256,2,576]{0,2,1:T(8,128)(2,1)} fusion(bf16[2,256,1024]{1,2,0:T(8,128)(2,1)S(1)} %fusion.2, bf16[512,576]{0,1:T(8,128)(2,1)} %collective-permute-done, bf16[512,576]{0,1:T(8,128)(2,1)} %copy-done.1), kind=kOutput, calls=%fused_computation.25 | convolution fusion | flops 606633984 | bytes 2818048 | tf_op jit(solution)/shard_map/htp,pd->thd/dot_general | solution.py:43
  101.2 18.4 %all-to-all-done.2 = bf16[64,8,576]{2,1,0:T(8,128)(2,1)S(1)} async-done(((bf16[64,8,576]{2,1,0:T(8,128)(2,1)}), bf16[64,8,576]{2,1,0:T(8,128)(2,1)S(1)}, u32[]{:S(2)}, u32[]{:S(2)}) %all-to-all-start.2) | async-done | bytes 589856 | tf_op jit(solution)/shard_map/all_to_all | solution.py:21
  119.6 0.8 convert_reduce_fusion
  (23 shorter events, 1.0 us)
Async XLA Ops:
  0.6 33.4 %copy-start = (bf16[256,2,576]{0,2,1:T(8,128)(2,1)S(1)}, bf16[256,2,576]{0,2,1:T(8,128)(2,1)}, u32[]{:S(2)}) copy-start(bf16[256,2,576]{0,2,1:T(8,128)(2,1)} %param.8) | copy-start | bytes 1769476
  0.6 31.2 %copy-start.6 = (f32[16]{0:T(128)S(1)}, f32[16]{0:T(128)}, u32[]{:S(2)}) copy-start(f32[16]{0:T(128)} %param.12) | copy-start | bytes 196
  0.7 31.3 %copy-start.5 = (s32[256]{0:T(256)S(1)}, s32[256]{0:T(256)}, u32[]{:S(2)}) copy-start(s32[256]{0:T(256)} %param.13) | copy-start | bytes 3076
  0.7 31.4 %copy-start.2 = (bf16[256,2,512]{2,1,0:T(2,128)(2,1)S(1)}, bf16[256,2,512]{2,1,0:T(2,128)(2,1)}, u32[]{:S(2)}) copy-start(bf16[256,2,512]{2,1,0:T(2,128)(2,1)} %param.10) | copy-start | bytes 1572868
  0.7 31.3 %copy-start.3 = (bf16[256,2,512]{2,1,0:T(2,128)(2,1)S(1)}, bf16[256,2,512]{2,1,0:T(2,128)(2,1)}, u32[]{:S(2)}) copy-start(bf16[256,2,512]{2,1,0:T(2,128)(2,1)} %param.9) | copy-start | bytes 1572868
  2.6 27.1 %all-to-all-start = ((bf16[8,64,576]{2,1,0:T(8,128)(2,1)}), bf16[8,64,576]{2,1,0:T(8,128)(2,1)S(1)}, u32[]{:S(2)}, u32[]{:S(2)}) async-start(bf16[8,64,576]{2,1,0:T(8,128)(2,1)} %broadcast_in_dim.16), calls=%async_computation | async-start | bytes 1310720 | tf_op jit(solution)/shard_map/all_to_all | solution.py:21
  29.9 6.9 %copy-start.1 = (bf16[512,576]{0,1:T(8,128)(2,1)}, bf16[512,576]{0,1:T(8,128)(2,1)S(1)}, u32[]{:S(2)}) copy-start(bf16[512,576]{0,1:T(8,128)(2,1)S(1)} %copy.61) | copy-start | bytes 1769476
  29.9 4.1 %collective-permute-start = (bf16[512,576]{0,1:T(8,128)(2,1)S(1)}, bf16[512,576]{0,1:T(8,128)(2,1)}, u32[]{:S(2)}, u32[]{:S(2)}) collective-permute-start(bf16[512,576]{0,1:T(8,128)(2,1)S(1)} %copy.61), channel_id=1, source_target_pairs={{0,64},{64,0},{1,65},{65,1},{2,66},{66,2},{3,67},{67,3},{4,68},{68... | collective-permute-start | bytes 1769480 | tf_op jit(solution)/shard_map/ppermute | solution.py:17
  36.1 0.7 copy-start.4
  40.3 4.9 %collective-permute-start.1 = (f32[512,576]{0,1:T(8,128)S(1)}, f32[512,576]{0,1:T(8,128)S(1)}, u32[]{:S(2)}, u32[]{:S(2)}) collective-permute-start(f32[512,576]{0,1:T(8,128)S(1)} %fusion.9), channel_id=1, source_target_pairs={{0,64},{64,0},{1,65},{65,1},{2,66},{66,2},{3,67},{67,3},{4,68},{68... | collective-permute-start | bytes 3538952 | tf_op jit(solution)/shard_map/ppermute | solution.py:17
  76.5 43.1 %all-to-all-start.2 = ((bf16[64,8,576]{2,1,0:T(8,128)(2,1)}), bf16[64,8,576]{2,1,0:T(8,128)(2,1)S(1)}, u32[]{:S(2)}, u32[]{:S(2)}) async-start(bf16[64,8,576]{2,1,0:T(8,128)(2,1)} %broadcast_in_dim.19), calls=%async_computation.2 | async-start | bytes 1310720 | tf_op jit(solution)/shard_map/all_to_all | solution.py:21

commit v2 on v1

v2 whole, which is shorter than its diff:
```python
import math

import jax
import jax.numpy as jnp
from jax import lax
from jax.experimental import pallas as pl
from jax.experimental.pallas import tpu as pltpu
from jax.sharding import Mesh, PartitionSpec as P

ROPE = 64
NOPE = 128
VMEM_BYTES = 20 * 1024 * 1024


def softmax_scale():
    return (0.1 * math.log(40.0) + 1.0) ** 2 / math.sqrt(NOPE + ROPE)


def to_partner(value):
    return lax.ppermute(value, "core", [(0, 1), (1, 0)])


def exchanged(pieces, axes):
    return lax.all_to_all(pieces, axes, 0, 0, tiled=True)


def dot(a, b, dims=((1,), (0,))):
    return lax.dot_general(a, b, (dims, ((), ())), preferred_element_type=jnp.float32)


def key_grad(score_grad, weights, queries, scaled, out_ref):
    value_width = scaled.shape[-1]
    key_term = dot(score_grad, queries)
    owners, rows, _ = out_ref.shape
    value_term = key_term[:, :value_width] + dot(weights, scaled)
    out_ref[:, :, :value_width] = value_term.reshape(owners, rows, value_width)
    out_ref[:, :, value_width:] = key_term[:, value_width:].reshape(owners, rows, -1)


def joined(keys):
    return keys[...].reshape(-1, keys.shape[-1])


def scores_of(keys, queries_t, scaled_t):
    return (
        softmax_scale() * dot(keys, queries_t),
        dot(keys[:, : scaled_t.shape[0]], scaled_t),
    )


def scores_kernel(mine, queries_t, scaled_t, scores, prob_grad):
    heads, _, slots = queries_t.shape
    keys = joined(mine)
    for h in range(heads):
        columns = pl.ds(h * slots, slots)
        scores[:, columns], prob_grad[:, columns] = scores_of(keys, queries_t[h], scaled_t[h])


def softmax_kernel(
    other, my_scores, my_prob_grad, queries_t, scaled_t, queries, scaled, suffix_dot, suffix_lse,
    sent_grad, score_grad, weights,
):
    factor = softmax_scale()
    heads, _, slots = queries_t.shape
    half = other.shape[0] * other.shape[1]
    keys = joined(other)
    other_weights = []
    for h in range(heads):
        columns = pl.ds(h * slots, slots)
        other_scores, other_prob_grad = scores_of(keys, queries_t[h], scaled_t[h])
        scores = (my_scores[:, columns], other_scores)
        prob_grad = (my_prob_grad[:, columns], other_prob_grad)
        row_max = jnp.maximum(*[jnp.max(s, axis=0, keepdims=True) for s in scores])
        powers = [jnp.exp(s - row_max) for s in scores]
        total = sum(jnp.sum(p, axis=0, keepdims=True) for p in powers)
        prefix_lse = row_max + jnp.log(total)
        tail_lse = suffix_lse[h : h + 1, :]
        joint_max = jnp.maximum(prefix_lse, tail_lse)
        total_lse = joint_max + jnp.log(
            jnp.exp(prefix_lse - joint_max) + jnp.exp(tail_lse - joint_max)
        )
        share = jnp.exp(row_max - total_lse)
        prefix_dot = sum(
            jnp.sum(p * g, axis=0, keepdims=True) for p, g in zip(powers, prob_grad)
        )
        row_delta = share * prefix_dot + jnp.exp(tail_lse - total_lse) * suffix_dot[h : h + 1, :]
        for i in range(2):
            probability = powers[i] * share
            grad = factor * probability * (prob_grad[i] - row_delta)
            score_grad[pl.ds(i * half, half), columns] = grad.astype(jnp.bfloat16)
            if i == 0:
                weights[:, columns] = probability.astype(jnp.bfloat16)
            else:
                other_weights.append(probability.astype(jnp.bfloat16))
    key_grad(
        score_grad[pl.ds(half, half), :],
        jnp.concatenate(other_weights, axis=1),
        queries[...],
        scaled[...],
        sent_grad,
    )


def rest_kernel(
    mine, other, queries, scaled, score_grad, weights, kept_grad, query_grad_t
):
    half = mine.shape[0] * mine.shape[1]
    heads, _, slots = query_grad_t.shape
    key_grad(score_grad[:half, :], weights[...], queries[...], scaled[...], kept_grad)
    rows = ((0,), (0,))
    query_grad = dot(joined(mine), score_grad[:half, :], rows)
    query_grad += dot(joined(other), score_grad[pl.ds(half, half), :], rows)
    for h in range(heads):
        query_grad_t[h] = query_grad[:, h * slots : (h + 1) * slots].astype(jnp.bfloat16)


def call(kernel, name, outs, *args):
    return pl.pallas_call(
        kernel,
        out_shape=outs,
        name=name,
        compiler_params=pltpu.CompilerParams(vmem_limit_bytes=VMEM_BYTES),
    )(*args)


def prepared(queries, cotangent, suffix_out, suffix_lse, rewards, slot_sample):
    slots, heads, width = queries.shape
    centred = rewards - jnp.mean(rewards)
    advantage_table = jnp.concatenate([centred, jnp.zeros((1,), jnp.float32)])
    sample_ids = jnp.arange(advantage_table.shape[0], dtype=jnp.int32)
    weight = jnp.sum(
        jnp.where(slot_sample[:, None] == sample_ids[None, :], advantage_table[None, :], 0.0),
        axis=1,
    )
    scaled = (weight[:, None, None] * cotangent.astype(jnp.float32)).astype(jnp.bfloat16)
    suffix_dot = jnp.sum(scaled.astype(jnp.float32) * suffix_out.astype(jnp.float32), axis=2)
    return (
        jnp.transpose(queries, (1, 2, 0)),
        jnp.transpose(scaled, (1, 2, 0)),
        jnp.transpose(queries, (1, 0, 2)).reshape(heads * slots, width),
        jnp.transpose(scaled, (1, 0, 2)).reshape(heads * slots, -1),
        suffix_dot.T,
        suffix_lse.astype(jnp.float32).T,
    )


def scores_part(mine, ready):
    queries_t, scaled_t = ready[:2]
    heads, _, slots = queries_t.shape
    out = jax.ShapeDtypeStruct((mine.shape[0] * mine.shape[1], heads * slots), jnp.float32)
    return call(scores_kernel, "scores", (out, out), mine, queries_t, scaled_t)


def softmax_part(other, my_scores, ready):
    queries_t, scaled_t, queries_r, scaled_r, suffix_dot, tail_lse = ready
    heads, _, slots = queries_t.shape
    half = other.shape[0] * other.shape[1]
    return call(
        softmax_kernel,
        "softmax",
        (
            jax.ShapeDtypeStruct(other.shape, jnp.float32),
            jax.ShapeDtypeStruct((2 * half, heads * slots), jnp.bfloat16),
            jax.ShapeDtypeStruct((half, heads * slots), jnp.bfloat16),
        ),
        other, *my_scores, queries_t, scaled_t, queries_r, scaled_r, suffix_dot, tail_lse,
    )


def rest_part(mine, other, ready, score_grad, weights):
    queries_t, _, queries_r, scaled_r, _, _ = ready
    return call(
        rest_kernel,
        "rest",
        (
            jax.ShapeDtypeStruct(mine.shape, jnp.float32),
            jax.ShapeDtypeStruct(queries_t.shape, jnp.bfloat16),
        ),
        mine, other, queries_r, scaled_r, score_grad, weights,
    )


def on_device(latent, queries, cotangent, suffix_out, suffix_lse, rewards, slot_sample):
    chips = lax.axis_size("x")
    ys, zs = lax.axis_size("y"), lax.axis_size("z")
    rows, width = latent.shape

    mine = exchanged(jnp.broadcast_to(latent[None], (chips, rows, width)), "x")
    ready = prepared(queries, cotangent, suffix_out, suffix_lse, rewards, slot_sample)
    mine, ready = lax.optimization_barrier((mine, ready))
    other = to_partner(mine)
    sent_grad, score_grad, weights = softmax_part(other, scores_part(mine, ready), ready)
    received = to_partner(sent_grad)
    kept_grad, query_grad_t = rest_part(mine, other, ready, score_grad, weights)
    on_chip = (kept_grad + received).astype(jnp.bfloat16)

    pieces = exchanged(on_chip.reshape(chips * ys, rows // ys, width), ("x", "y"))
    part = jnp.sum(pieces.astype(jnp.float32), axis=0).astype(jnp.bfloat16)
    copies = exchanged(jnp.broadcast_to(part[None], (ys * zs, *part.shape)), ("y", "z"))
    copies = copies.reshape(ys, zs, rows // ys, width).astype(jnp.float32)
    latent_grad = jnp.sum(copies, axis=1).reshape(rows, width)
    return jnp.transpose(query_grad_t, (2, 0, 1)), latent_grad


def solution(mesh):
    prompt, sample = mesh.devices.shape
    side = math.isqrt(sample)
    grid = Mesh(
        mesh.devices.reshape(prompt // 2, 2, side, sample // side), ("x", "core", "y", "z")
    )
    slots, heads = ("x", "core"), ("y", "z")
    in_specs = (
        P(slots, None),
        P(slots, heads, None),
        P(slots, heads, None),
        P(slots, heads, None),
        P(slots, heads),
        P(),
        P(slots),
    )
    out_specs = (P(slots, heads, None), P(slots, None))
    return jax.shard_map(
        on_device, mesh=grid, in_specs=in_specs, out_specs=out_specs, check_vma=False
    )
```

time: 121 us -> 114 us (0.942)
  blocking collectives: 29.5 us -> 71.5 us
  starting transfers between devices: 32.9 us -> 10.9 us
  waiting for transfers between devices: 38.8 us -> 18.1 us
  matrix products: 8.79 us -> 0 us
  Pallas kernels: 0 us -> 5.98 us
  other arithmetic: 4.63 us -> 2.02 us
    all_to_all x1 -> x2, blocking collectives: 29.5 us -> 71.5 us  [exchanged(): return lax.all_to_all(pieces, axes, 0, 0, tiled=True)]
    all_to_all x2 -> x1, starting transfers between devices: 28.6 us -> 6.89 us  [exchanged(): return lax.all_to_all(pieces, axes, 0, 0, tiled=True)]
    all_to_all x2 -> x1, waiting for transfers between devices: 36.8 us -> 16.3 us  [exchanged(): return lax.all_to_all(pieces, axes, 0, 0, tiled=True)]
    dot_general x7 -> x0, matrix products: 8.79 us -> none  [the longest x1 2.84 us: query_grad(): jnp.einsum('htp,pd->thd', score_grad, keys, preferred_element_type=jnp.fl...]
    pallas_call x0 -> x3, Pallas kernels: none -> 5.98 us  [call(): pl.pallas_call(kernel, out_shape=outs, name=name, compiler_params=pltpu.C...]
    reduce_sum x4 -> x3, other arithmetic: 3.06 us -> 0.89 us  [the longest x1 0.6 us: prepared(): centred = rewards - jnp.mean(rewards)]
    unnamed x14, local copies, waits for them, and re-layouts: 0.34 us -> 1.74 us
  transfers between devices with their start and end apart: 4 -> 3, of which waited for: 3 -> 3; matrix products, arithmetic and copies ran while one was open for 6% -> 2% of each run, Pallas kernels for 0% -> 3%
where the time goes in v2:
time: 114 us
  blocking collectives  71.5 us (63%)
  waiting for transfers between devices  18.1 us (16%)
  starting transfers between devices  10.9 us (10%)
  Pallas kernels  5.98 us (5%)
  local copies, waits for them, and re-layouts  4.13 us (4%)
  other arithmetic  2.02 us (2%)
  between operations  1.42 us (1%)
    all_to_all x2, blocking collectives, exchanged(): return lax.all_to_all(pieces, axes, 0, 0, tiled=True)  71.5 us
    all_to_all x1, waiting for transfers between devices, exchanged(): return lax.all_to_all(pieces, axes, 0, 0, tiled=True)  16.3 us
    all_to_all x1, starting transfers between devices, exchanged(): return lax.all_to_all(pieces, axes, 0, 0, tiled=True)  6.89 us
    pallas_call x3, Pallas kernels, call(): pl.pallas_call(kernel, out_shape=outs, name=name, compiler_params=pltpu.C...  5.98 us
    ppermute x2, starting transfers between devices, to_partner(): return lax.ppermute(value, 'core', [(0, 1), (1, 0)])  3.96 us
  transfers between devices with their start and end apart: 3, of which 3 were waited for; matrix products, arithmetic and copies ran while one was open for 2% of the time, Pallas kernels for 3%

profile of v2, /device:TPU:32, one launch (start us, length us, event | category | flops | bytes accessed | tf_op | source)
XLA Modules:
  0.0 114.1 jit_solution(1231743758298709399)
XLA Ops:
  0.6 1.8 %broadcast_in_dim.16 = bf16[8,64,576]{2,1,0:T(8,128)(2,1)} broadcast(bf16[64,576]{1,0:T(8,128)(2,1)} %param.7), dimensions={1,2} | broadcast | bytes 663552 | tf_op jit(solution)/shard_map/broadcast_in_dim | solution.py:188
  2.5 6.9 %all-to-all-start = ((bf16[8,64,576]{2,1,0:T(8,128)(2,1)}), bf16[8,64,576]{2,1,0:T(8,128)(2,1)S(1)}, u32[]{:S(2)}, u32[]{:S(2)}) async-start(bf16[8,64,576]{2,1,0:T(8,128)(2,1)} %broadcast_in_dim.16), calls=%async_computation | async-start | bytes 1310720 | tf_op jit(solution)/shard_map/all_to_all | solution.py:24
  9.4 0.5 copy.13
  10.0 0.5 copy.16
  10.5 0.6 reduce_sum.48
  11.8 0.1 pad_maximum_fusion
  11.9 0.1 select_reduce_fusion
  11.9 0.2 multiply_reduce_fusion
  12.2 0.2 copy.15
  12.4 0.6 copy-done
  13.0 0.3 copy.14
  13.3 16.3 %all-to-all-done.mine = bf16[8,64,576]{2,1,0:T(8,128)(2,1)S(1)} async-done(((bf16[8,64,576]{2,1,0:T(8,128)(2,1)}), bf16[8,64,576]{2,1,0:T(8,128)(2,1)S(1)}, u32[]{:S(2)}, u32[]{:S(2)}) %all-to-all-start) | async-done | bytes 589856 | tf_op jit(solution)/shard_map/all_to_all | solution.py:24
  29.7 1.9 %collective-permute-start = (bf16[8,64,576]{2,1,0:T(8,128)(2,1)S(1)}, bf16[8,64,576]{2,1,0:T(8,128)(2,1)S(1)}, u32[]{:S(2)}, u32[]{:S(2)}) collective-permute-start(bf16[8,64,576]{2,1,0:T(8,128)(2,1)S(1)} %all-to-all-done.mine), channel_id=1, source_target_pairs={{0,64},{64,0},{1,65},{65,1},{2,66},{66,2},{3,67},{67,3},{4,68},{68... | collective-permute-start | bytes 1769480 | tf_op jit(solution)/shard_map/ppermute | solution.py:20
  31.6 0.8 scores.1
  32.4 1.2 %collective-permute-done.other = bf16[8,64,576]{2,1,0:T(8,128)(2,1)S(1)} collective-permute-done((bf16[8,64,576]{2,1,0:T(8,128)(2,1)S(1)}, bf16[8,64,576]{2,1,0:T(8,128)(2,1)S(1)}, u32[]{:S(2)}, u32[]{:S(2)}) %collective-permute-start) | collective-permute-done | bytes 589856 | tf_op jit(solution)/shard_map/ppermute | solution.py:20
  33.6 2.9 %softmax.1 = (f32[8,64,576]{2,1,0:T(8,128)S(1)}, bf16[1024,512]{1,0:T(8,128)(2,1)S(1)}, bf16[512,512]{1,0:T(8,128)(2,1)S(1)}) custom-call(bf16[8,64,576]{2,1,0:T(8,128)(2,1)S(1)} %collective-permute-done.other, f32[512,512]{1,0:T(8,128)S(1)} %get-tuple-element.21.my_scores, f32[512,512]{1,0:T(8,128)S(1)} %get-tuple-element.22.my_prob_grad, ...), custom_call_target="tpu_custom_call" | custom-call | tf_op jit(solution)/shard_map/softmax/pallas_call | solution.py:118
  36.5 2.0 %collective-permute-start.1 = (f32[8,64,576]{2,1,0:T(8,128)S(1)}, f32[8,64,576]{2,1,0:T(8,128)S(1)}, u32[]{:S(2)}, u32[]{:S(2)}) collective-permute-start(f32[8,64,576]{2,1,0:T(8,128)S(1)} %get-tuple-element.29), channel_id=1, source_target_pairs={{0,64},{64,0},{1,65},{65,1},{2,66},{66,2},{3,67},{67,3},{4,68},{68... | collective-permute-start | bytes 3538952 | tf_op jit(solution)/shard_map/ppermute | solution.py:20
  38.6 2.3 %rest.1 = (f32[8,64,576]{2,1,0:T(8,128)S(1)}, bf16[2,576,256]{2,1,0:T(8,128)(2,1)}) custom-call(bf16[8,64,576]{2,1,0:T(8,128)(2,1)S(1)} %all-to-all-done.mine, bf16[8,64,576]{2,1,0:T(8,128)(2,1)S(1)} %collective-permute-done.other, bf16[512,576]{1,0:T(8,128)(2,1)S(1)} %bitcast.18, bf16[512,512]{1,0:T(8,128)(2,1)S(1)} %bitcast.23, ...), custom_call_target="tpu_custom_call" | custom-call | tf_op jit(solution)/shard_map/rest/pallas_call | solution.py:118
  40.8 0.6 collective-permute-done.1
  41.4 0.1 add_convert_fusion
  41.6 29.3 %all_to_all.15 = bf16[64,8,576]{2,1,0:T(8,128)(2,1)S(1)} all-to-all(bf16[64,8,576]{2,1,0:T(8,128)(2,1)S(1)} %bitcast.25), channel_id=1, replica_groups=mesh['x'=8,'core'=2,'y'=8,'z'=8] {'x','y'}, dimensions={0} | all-to-all | bytes 1179648 | tf_op jit(solution)/shard_map/all_to_all | solution.py:24
  70.9 0.1 reduce_sum.51
  71.1 42.2 %all_to_all.16 = bf16[64,8,576]{2,1,0:T(8,128)(2,1)S(1)} all-to-all(bf16[64,8,576]{2,1,0:T(8,128)(2,1)S(1)} %broadcast_in_dim.19), channel_id=1, replica_groups=mesh['x'=8,'core'=2,'y'=8,'z'=8] {'y','z'}, dimensions={0} | all-to-all | bytes 1179648 | tf_op jit(solution)/shard_map/all_to_all | solution.py:24
  113.3 0.8 convert_reduce_fusion
  (14 shorter events, 0.1 us)
Async XLA Ops:
  0.6 8.7 %copy-start.1 = (bf16[256,2,512]{2,1,0:T(2,128)(2,1)S(1)}, bf16[256,2,512]{2,1,0:T(2,128)(2,1)}, u32[]{:S(2)}) copy-start(bf16[256,2,512]{2,1,0:T(2,128)(2,1)} %param.9) | copy-start | bytes 1572868
  2.5 7.5 %copy-start.2 = (bf16[256,2,512]{2,1,0:T(2,128)(2,1)S(1)}, bf16[256,2,512]{2,1,0:T(2,128)(2,1)}, u32[]{:S(2)}) copy-start(bf16[256,2,512]{2,1,0:T(2,128)(2,1)} %param.10) | copy-start | bytes 1572868
  2.5 27.2 %all-to-all-start = ((bf16[8,64,576]{2,1,0:T(8,128)(2,1)}), bf16[8,64,576]{2,1,0:T(8,128)(2,1)S(1)}, u32[]{:S(2)}, u32[]{:S(2)}) async-start(bf16[8,64,576]{2,1,0:T(8,128)(2,1)} %broadcast_in_dim.16), calls=%async_computation | async-start | bytes 1310720 | tf_op jit(solution)/shard_map/all_to_all | solution.py:24
  9.4 1.1 copy-start.5
  9.4 2.5 %copy-start.4 = (s32[256]{0:T(256)S(1)}, s32[256]{0:T(256)}, u32[]{:S(2)}) copy-start(s32[256]{0:T(256)} %param.13) | copy-start | bytes 3076
  11.9 1.1 copy-start
  12.2 1.2 %copy-start.3 = (bf16[256,2]{0,1:T(2,128)(2,1)S(1)}, bf16[256,2]{0,1:T(2,128)(2,1)}, u32[]{:S(2)}) copy-start(bf16[256,2]{0,1:T(2,128)(2,1)} %param.11) | copy-start | bytes 3076
  29.7 4.0 %collective-permute-start = (bf16[8,64,576]{2,1,0:T(8,128)(2,1)S(1)}, bf16[8,64,576]{2,1,0:T(8,128)(2,1)S(1)}, u32[]{:S(2)}, u32[]{:S(2)}) collective-permute-start(bf16[8,64,576]{2,1,0:T(8,128)(2,1)S(1)} %all-to-all-done.mine), channel_id=1, source_target_pairs={{0,64},{64,0},{1,65},{65,1},{2,66},{66,2},{3,67},{67,3},{4,68},{68... | collective-permute-start | bytes 1769480 | tf_op jit(solution)/shard_map/ppermute | solution.py:20
  36.5 4.9 %collective-permute-start.1 = (f32[8,64,576]{2,1,0:T(8,128)S(1)}, f32[8,64,576]{2,1,0:T(8,128)S(1)}, u32[]{:S(2)}, u32[]{:S(2)}) collective-permute-start(f32[8,64,576]{2,1,0:T(8,128)S(1)} %get-tuple-element.29), channel_id=1, source_target_pairs={{0,64},{64,0},{1,65},{65,1},{2,66},{66,2},{3,67},{67,3},{4,68},{68... | collective-permute-start | bytes 3538952 | tf_op jit(solution)/shard_map/ppermute | solution.py:20
